TPU v7x, 32 devices: a whole 2x2x4 slice. The times are simulated.
32 devices in a mesh: plant: 2 (over x), section: 16 (over z, y, core).
Axes of the slice: x: 2, y: 2, z: 4, core: 2. Of those that a mesh axis runs over, the one named last changes fastest.
Arguments:
- dynamics_operator: bfloat16 [1024, 512], P('plant'), parts along dimension 0
- control_gain_array: bfloat16 [1024, 256], P('plant'), parts along dimension 0
- kkt_inverse: bfloat16 [1536, 768], P('plant'), parts along dimension 0
- lin_state: float32 [1024, 4096], P(('plant', 'section')), parts along dimension 0, may hold values from -6 to 6
- lin_input: float32 [512, 4096], P(('plant', 'section')), parts along dimension 0, may hold values from -6 to 6
- block_start: int32 [2], P('plant'), parts along dimension 0, may hold values from 0 to 15
- period: int32 [2], P('plant'), parts along dimension 0, may hold values from 2048 to 4096
Outputs:
- state_traj: float32 [1024, 4096], P('plant', 'section'), parts along dimension 0
- input_traj: float32 [512, 4096], P('plant', 'section'), parts along dimension 0
- consensus: float32 [1024, 4096], P('plant', 'section'), parts along dimension 0
- residual_norms: float32 [4], P('plant'), parts along dimension 0
There are 2 independent parts, one for each index of `plant`. A program takes and returns all parts, laid end to end along the dimension named above; each array names one. Nothing has to cross between parts.
Inputs may be any that keep to these rules, and one draw needn't show every extreme that they name: Device d of the section axis holds the block of logical sections starting at 256 * ((d - block_start) mod the axis's size).
All inputs are finite; a program needn't handle non-finite values.
Results may differ from a plain program's by a relative error of at most 0.0045.
Values sent between devices are 32-bit elements; how exact they have to be, the bound alone decides.
A program may use at most 64 MiB of HBM per device.

v0:
```python
import functools

import jax
import jax.numpy as jnp
from jax import lax
from jax.experimental import pallas as pl
from jax.experimental.pallas import tpu as pltpu
from jax.sharding import PartitionSpec as P

ITERS = 4
RHO = 1.0
LANES = 128
CHUNK = 512
ROWS = 64
PARTS = 2
NT = (((1,), (1,)), ((), ()))


def dot(a, b):
    return jnp.dot(a, b, preferred_element_type=jnp.float32)


def partner(me, k, n, sign):
    if n & (n - 1):
        return lax.rem(me + sign * k + n, n)
    other = me
    for bit in range(n.bit_length()):
        if (k >> bit) & 1:
            other = other + (1 - 2 * ((me // (1 << bit)) % 2)) * (1 << bit)
    return other


def kernel(
    n, width,
    a_hbm, b_hbm, k_hbm, cs_hbm, ci_hbm, start_ref, period_ref,
    x_out, u_out, z_out, norm_out,
    ab, gt, kkt, cs, ci, recv_s, recv_i, cpad, hsend, recv_h, hcol,
    negc, rhs, w, wb, pred, y, v, z, g, xo, uo, zo, part, recv_p,
    load_sem, own_sem, send_sem, recv_sem, out_sem,
):
    me = lax.axis_index("section")
    nx = a_hbm.shape[0]
    nu = b_hbm.shape[1]
    rs, ri = cs.shape[0], ci.shape[0]
    pw = width // PARTS
    ext = pw + LANES
    shift = LANES // PARTS
    start = start_ref[0]
    period = period_ref[0]

    def cols(i, h):
        return pl.ds(pl.multiple_of(i * width + h * pw, LANES), pw)

    loads = [
        pltpu.make_async_copy(cs_hbm, cs, load_sem.at[0]),
        pltpu.make_async_copy(ci_hbm, ci, load_sem.at[1]),
        pltpu.make_async_copy(a_hbm, ab.at[:, pl.ds(0, nx)], load_sem.at[2]),
        pltpu.make_async_copy(b_hbm, ab.at[:, pl.ds(nx, nu)], load_sem.at[3]),
        pltpu.make_async_copy(k_hbm, kkt, load_sem.at[4]),
    ]
    for h in range(PARTS):
        loads += [
            pltpu.make_async_copy(
                cs_hbm.at[:, cols(me, h)], recv_s.at[h, me], load_sem.at[5 + 2 * h]
            ),
            pltpu.make_async_copy(
                ci_hbm.at[:, cols(me, h)], recv_i.at[h, me], load_sem.at[6 + 2 * h]
            ),
        ]
    for c in loads:
        c.start()

    barrier = pltpu.get_barrier_semaphore()
    for k in range(1, n):
        pl.semaphore_signal(barrier, inc=1, device_id={"section": partner(me, k, n, 1)})
    pl.semaphore_wait(barrier, n - 1)

    loads[0].wait()
    loads[1].wait()

    def copies(kind, k, incoming=False):
        to = partner(me, k, n, 1)
        if kind == 0:
            src, dst = part, recv_p
        elif kind == 1:
            src, dst = hsend.at[to], recv_h
        elif kind % 2 == 0:
            src, dst = cs.at[:, cols(to, kind // 2 - 1)], recv_s.at[kind // 2 - 1]
        else:
            src, dst = ci.at[:, cols(to, kind // 2 - 1)], recv_i.at[kind // 2 - 1]
        slot = partner(me, k, n, -1) if incoming else me
        return pltpu.make_async_remote_copy(
            src_ref=src, dst_ref=dst.at[slot], send_sem=send_sem.at[kind, k],
            recv_sem=recv_sem.at[kind, slot], device_id={"section": to},
        )

    order = list(range(1, n // 2)) + list(range(n - 1, n // 2 - 1, -1))
    for k in order:
        copies(2, k).start()
        copies(3, k).start()

    row = lax.broadcasted_iota(jnp.int32, (n * PARTS * 8, 1), 0)
    block = row // (PARTS * 8) - start
    block = jnp.where(block < 0, block + n, block)
    base = block * width + (row // 8) % PARTS * pw
    item = row % 8
    end = jnp.minimum(period - base, pw)
    ahead = base + end + item
    ahead = jnp.where(ahead >= period, ahead - period, ahead)
    behind = base + item - 8
    behind = jnp.where(behind < 0, behind + period, behind)
    place = jnp.where(item < ITERS, ahead, behind) + start * width
    place = jnp.where(place >= n * width, place - n * width, place)

    cpad[...] = jnp.zeros_like(cpad)

    def pick(j, total):
        at = pl.ds(pl.multiple_of(j * CHUNK, CHUNK), CHUNK)
        cpad[pl.ds(0, rs), :] = cs[:, at]
        cpad[pl.ds(rs, ri), :] = ci[:, at]
        column = lax.broadcasted_iota(jnp.int32, (n * PARTS * 8, CHUNK), 1) + j * CHUNK
        onehot = jnp.where(column == place, 1.0, 0.0).astype(jnp.bfloat16)
        rest = cpad[...]
        for _ in range(3):
            piece = rest.astype(jnp.bfloat16)
            rest = rest - piece.astype(jnp.float32)
            total = total + lax.dot_general(onehot, piece, NT, preferred_element_type=jnp.float32)
        return total

    picked = lax.fori_loop(
        0, cs.shape[1] // CHUNK, pick, jnp.zeros((n * PARTS * 8, LANES), jnp.float32)
    )
    picked = picked.reshape(n, PARTS, 8, LANES)
    packed = picked[:, 0].reshape(n * 8, LANES)
    for h in range(1, PARTS):
        packed = packed + pltpu.roll(picked[:, h].reshape(n * 8, LANES), h * shift, 1)
    hsend[...] = packed.reshape(n, 8, LANES)
    own_halo = pltpu.make_async_copy(hsend.at[me], recv_h.at[me], own_sem.at[0])
    own_halo.start()
    for k in order:
        copies(1, k).start()
    for h in range(1, PARTS):
        for k in order:
            copies(2 + 2 * h, k).start()
            copies(3 + 2 * h, k).start()

    loads[2].wait()
    loads[3].wait()
    loads[4].wait()
    gt[...] = ab[...].T

    own_halo.wait()
    for k in order:
        copies(1, k, True).wait_recv()

    flipped = recv_h[...].reshape(n * 8, LANES).T
    for s in range(n):
        tile = s * 8 // LANES * LANES
        piece = flipped[:, tile:tile + LANES]
        if s * 8 - tile:
            piece = pltpu.roll(piece, LANES - (s * 8 - tile), 1)
        for h in range(PARTS):
            top = h * shift
            hcol[h, pl.ds(s * rs, rs), :] = piece[top:top + rs]
            hcol[h, pl.ds(nx + s * ri, ri), :] = piece[top + rs:top + rs + ri]

    mine = me - start
    mine = jnp.where(mine < 0, mine + n, mine)
    lane = lax.broadcasted_iota(jnp.int32, (1, LANES), 1)
    primal = jnp.zeros((8, LANES), jnp.float32)
    dual = jnp.zeros((8, LANES), jnp.float32)

    def fold(value):
        total = jnp.zeros((8, LANES), jnp.float32)
        for a in range(0, value.shape[0], 8):
            for b in range(0, value.shape[1], LANES):
                total = total + value[a:a + 8, b:b + LANES]
        return total

    for h in range(PARTS):
        base = mine * width + h * pw
        finish = jnp.minimum(period - base, pw)
        own_cols = pl.ds(h * pw, pw)
        loads[5 + 2 * h].wait()
        loads[6 + 2 * h].wait()
        for k in order:
            copies(2 + 2 * h, k, True).wait_recv()
            copies(3 + 2 * h, k, True).wait_recv()

        for s in range(n):
            negc[pl.ds(s * rs, rs), pl.ds(0, pw)] = -recv_s[h, s]
            negc[pl.ds(nx + s * ri, ri), pl.ds(0, pw)] = -recv_i[h, s]
        for r in range(0, nx + nu, ROWS):
            at = pl.ds(r, ROWS)
            halo = -hcol[h, at, :]
            back = pltpu.roll(halo, LANES - 8, 1)
            fills = [jnp.broadcast_to(halo[:, i:i + 1], (ROWS, LANES)) for i in range(ITERS)]
            for t in range(0, ext, LANES):
                if t < pw:
                    value = negc[at, pl.ds(t, LANES)]
                else:
                    value = jnp.where(lane >= LANES - ITERS, back, 0.0)
                for i in range(ITERS):
                    value = jnp.where(lane + t == finish + i, fills[i], value)
                negc[at, pl.ds(t, LANES)] = value
                rhs[at, pl.ds(t, LANES)] = value.astype(jnp.bfloat16)

        ids = base + lax.broadcasted_iota(jnp.int32, (1, pw), 1)
        active = ids < period
        for it in range(ITERS):
            last = it == ITERS - 1
            if it > 0:
                w[...] = dot(gt[...], g[...])
                for r in range(0, nx + nu, ROWS):
                    at = pl.ds(r, ROWS)
                    if r < nx:
                        value = negc[at, :] + RHO * (z[at, :] - y[at, :]) + RHO * w[at, :]
                    else:
                        value = negc[at, :] + RHO * w[at, :]
                    rhs[at, :] = value.astype(jnp.bfloat16)
            w[...] = dot(kkt[...], rhs[...])
            for r in range(0, nx + nu, ROWS):
                at = pl.ds(r, ROWS)
                wb[at, :] = w[at, :].astype(jnp.bfloat16)
            pred[...] = dot(ab[...], wb[...])
            for r in range(0, nx, ROWS):
                at = pl.ds(r, ROWS)
                x = w[at, :]
                q = pred[at, :]
                own = x + y[at, :] if it else x
                link = q + v[at, :] if it else q
                znew = 0.5 * (own + pltpu.roll(link, 1, 1))
                znext = pltpu.roll(znew, ext - 1, 1)
                if not last:
                    y[at, :] = own - znew
                    vnew = link - znext
                    v[at, :] = vnew
                    g[at, :] = (znext - vnew).astype(jnp.bfloat16)
                    z[at, :] = znew
                else:
                    miss = (x - znew) ** 2 + (q - znext) ** 2
                    primal = primal + fold(jnp.where(active, miss[:, :pw], 0.0))
                    change = znew - z[at, :] if it else znew
                    dual = dual + fold(jnp.where(active, (change * change)[:, :pw], 0.0))
                    xo[at, own_cols] = jnp.where(active, x[:, :pw], 0.0)
                    zo[at, own_cols] = jnp.where(active, znew[:, :pw], 0.0)
        for r in range(0, nu, ROWS):
            uo[pl.ds(r, ROWS), own_cols] = jnp.where(
                active, w[pl.ds(nx + r, ROWS), pl.ds(0, pw)], 0.0
            )
    part[pl.ds(0, 8), :] = primal
    part[pl.ds(8, 8), :] = RHO * RHO * dual
    recv_p[me] = part[...]
    for k in order:
        copies(0, k).start()
    outs = [
        pltpu.make_async_copy(xo, x_out, out_sem.at[0]),
        pltpu.make_async_copy(uo, u_out, out_sem.at[1]),
        pltpu.make_async_copy(zo, z_out, out_sem.at[2]),
    ]
    for c in outs:
        c.start()
    for k in order:
        copies(0, k, True).wait_recv()
    total = recv_p[0]
    for s in range(1, n):
        total = total + recv_p[s]
    top = jnp.sqrt(jnp.broadcast_to(jnp.sum(total[:8], keepdims=True), (8, LANES)))
    low = jnp.sqrt(jnp.broadcast_to(jnp.sum(total[8:], keepdims=True), (8, LANES)))
    norm_out[0] = jnp.max(top)
    norm_out[1] = jnp.max(low)
    for c in outs:
        c.wait()
    for kind in range(2 + 2 * PARTS):
        for k in order:
            copies(kind, k).wait_send()


def local(a, b, kkt, lin_state, lin_input, block_start, period):
    n = lax.axis_size("section")
    width = lin_state.shape[1] // n
    pw = width // PARTS
    ext = pw + LANES
    nx, nu = b.shape
    nw = nx + nu
    rs, ri = lin_state.shape[0], lin_input.shape[0]
    f32, bf16 = jnp.float32, jnp.bfloat16
    anyspec = pl.BlockSpec(memory_space=pl.ANY)
    smem = pl.BlockSpec(memory_space=pltpu.SMEM)
    vmem = pltpu.VMEM
    return pl.pallas_call(
        functools.partial(kernel, n, width),
        name="admm",
        out_shape=(
            jax.ShapeDtypeStruct((nx, width), f32),
            jax.ShapeDtypeStruct((nu, width), f32),
            jax.ShapeDtypeStruct((nx, width), f32),
            jax.ShapeDtypeStruct((2,), f32),
        ),
        in_specs=[anyspec] * 5 + [smem] * 2,
        out_specs=(anyspec, anyspec, anyspec, smem),
        scratch_shapes=[
            vmem((nx, nw), bf16), vmem((nw, nx), bf16), vmem((nw, nw), bf16),
            vmem(lin_state.shape, f32), vmem(lin_input.shape, f32),
            vmem((PARTS, n, rs, pw), f32), vmem((PARTS, n, ri, pw), f32),
            vmem((LANES, CHUNK), f32),
            vmem((n, 8, LANES), f32), vmem((n, 8, LANES), f32), vmem((PARTS, nw, LANES), f32),
            vmem((nw, ext), f32), vmem((nw, ext), bf16), vmem((nw, ext), f32),
            vmem((nw, ext), bf16), vmem((nx, ext), f32),
            vmem((nx, ext), f32), vmem((nx, ext), f32), vmem((nx, ext), f32),
            vmem((nx, ext), bf16),
            vmem((nx, width), f32), vmem((nu, width), f32), vmem((nx, width), f32),
            vmem((16, LANES), f32), vmem((n, 16, LANES), f32),
            pltpu.SemaphoreType.DMA((5 + 2 * PARTS,)), pltpu.SemaphoreType.DMA((1,)),
            pltpu.SemaphoreType.DMA((2 + 2 * PARTS, n)), pltpu.SemaphoreType.DMA((2 + 2 * PARTS, n)),
            pltpu.SemaphoreType.DMA((3,)),
        ],
        compiler_params=pltpu.CompilerParams(
            collective_id=0, has_side_effects=True, vmem_limit_bytes=62000000
        ),
    )(a, b, kkt, lin_state, lin_input, block_start, period)


def solution(mesh):
    return jax.shard_map(
        local,
        mesh=mesh,
        in_specs=(
            P("plant", None),
            P("plant", None),
            P("plant", None),
            P(("plant", "section"), None),
            P(("plant", "section"), None),
            P("plant"),
            P("plant"),
        ),
        out_specs=(P("plant", "section"), P("plant", "section"), P("plant", "section"), P("plant")),
        check_vma=False,
    )
```

profile of v0, /device:TPU:0, one launch (start us, length us, event | category | flops | bytes accessed | tf_op | source)
XLA Modules:
  0.0 47.6 jit_solution(6376472331389620053)
XLA Ops:
  1.9 41.7 %admm.1 = (f32[512,256]{1,0:T(8,128)}, f32[256,256]{1,0:T(8,128)}, f32[512,256]{1,0:T(8,128)}, f32[2]{0:T(128)}) custom-call(bf16[512,512]{1,0:T(8,128)(2,1)} %a_hbm.1, bf16[512,256]{1,0:T(8,128)(2,1)} %b_hbm.1, bf16[768,768]{1,0:T(8,128)(2,1)} %k_hbm.1, f32[32,4096]{1,0:T(8,128)} %cs_hbm.1, f32[16,4096]{1,0:T(8,128)} %ci_hbm.1, s32[1]{0:T(128)S(6)} %copy.15.start_ref, ...), custom_call_target="tpu_custom_call" | custom-call | tf_op jit(solution)/shard_map/admm/pallas_call | solution.py:291
  43.6 0.0 copy-start.1
  43.7 0.0 copy-start
  43.7 0.0 copy-start.2
  43.7 1.9 %copy.17 = f32[512,256]{1,0:T(8,128)} copy(f32[512,256]{1,0:T(8,128)} %get-tuple-element.8) | data formatting | bytes 1048576
  45.6 0.0 copy-done.1
  45.6 0.7 %copy.18 = f32[256,256]{1,0:T(8,128)} copy(f32[256,256]{1,0:T(8,128)S(1)} %copy-done.1) | data formatting | bytes 524288
  46.3 0.0 copy-done
  46.3 0.8 %copy.19 = f32[512,256]{1,0:T(8,128)} copy(f32[512,256]{1,0:T(8,128)S(1)} %copy-done) | data formatting | bytes 1048576
  47.1 0.0 copy-done.2
  47.1 0.5 %copy.20 = f32[2]{0:T(128)} copy(f32[2]{0:T(128)S(1)} %copy-done.2) | data formatting | bytes 16
Async XLA Ops:
  43.6 2.0 %copy-start.1 = (f32[256,256]{1,0:T(8,128)S(1)}, f32[256,256]{1,0:T(8,128)}, u32[]{:S(2)}) copy-start(f32[256,256]{1,0:T(8,128)} %get-tuple-element.9) | copy-start | bytes 786436
  43.7 2.7 %copy-start = (f32[512,256]{1,0:T(8,128)S(1)}, f32[512,256]{1,0:T(8,128)}, u32[]{:S(2)}) copy-start(f32[512,256]{1,0:T(8,128)} %get-tuple-element.10) | copy-start | bytes 1572868
  43.7 3.5 %copy-start.2 = (f32[2]{0:T(128)S(1)}, f32[2]{0:T(128)}, u32[]{:S(2)}) copy-start(f32[2]{0:T(128)} %get-tuple-element.11) | copy-start | bytes 28
where the time goes:
time: 47.8 us; the launch traced here: 47.6 us
  Pallas kernels  41.7 us (87%)
  local copies, waits for them, and re-layouts  3.96 us (8%)
  between operations  1.96 us (4%)
    pallas_call x1, Pallas kernels, local(): pl.pallas_call(functools.partial(kernel, n, width), name='admm', out_shap...  41.7 us
    unnamed x10, local copies, waits for them, and re-layouts  3.96 us

commit v1 on v0

v1 whole, which is shorter than its diff:
```python
import functools

import jax
import jax.numpy as jnp
from jax import lax
from jax.experimental import pallas as pl
from jax.experimental.pallas import tpu as pltpu
from jax.sharding import PartitionSpec as P

ITERS = 4
RHO = 1.0
LANES = 128
SUB = 8
CHUNK = 512
TILE = 256
ROWS = 16
NT = (((1,), (1,)), ((), ()))


def dot(a, b):
    return jnp.dot(a, b, preferred_element_type=jnp.float32)


def scaled(value):
    return value if RHO == 1.0 else RHO * value


def partner(me, k, n, sign):
    if n & (n - 1):
        return lax.rem(me + sign * k + n, n)
    other = me
    for bit in range(n.bit_length()):
        if (k >> bit) & 1:
            other = other + (1 - 2 * ((me // (1 << bit)) % 2)) * (1 << bit)
    return other


def kernel(
    n, width,
    a_hbm, b_hbm, k_hbm, cs_hbm, ci_hbm, start_hbm, period_hbm,
    x_out, u_out, z_out, norm_out,
    ab, abt, kkt, kt, cs, ci, recv_s, recv_i, cpad, hsend, recv_h, hrow,
    negc, rhs, w, wb, pred, link, zn, y, v, c, z, g, xo, uo, zo, part, recv_p,
    start_ref, period_ref,
    load_sem, send_sem, recv_sem, out_sem,
):
    me = lax.axis_index("section")
    nx = a_hbm.shape[0]
    nu = b_hbm.shape[1]
    nw = nx + nu
    rs, ri = cs.shape[0], ci.shape[0]
    rows = width + 2 * SUB
    half = LANES // 2

    def cols(i):
        return pl.ds(pl.multiple_of(i * width, LANES), width)

    loads = [
        pltpu.make_async_copy(cs_hbm, cs, load_sem.at[0]),
        pltpu.make_async_copy(ci_hbm, ci, load_sem.at[1]),
        pltpu.make_async_copy(start_hbm, start_ref, load_sem.at[2]),
        pltpu.make_async_copy(period_hbm, period_ref, load_sem.at[3]),
        pltpu.make_async_copy(a_hbm, ab.at[:, pl.ds(0, nx)], load_sem.at[4]),
        pltpu.make_async_copy(b_hbm, ab.at[:, pl.ds(nx, nu)], load_sem.at[5]),
        pltpu.make_async_copy(k_hbm, kkt, load_sem.at[6]),
        pltpu.make_async_copy(cs_hbm.at[:, cols(me)], recv_s.at[me], load_sem.at[7]),
        pltpu.make_async_copy(ci_hbm.at[:, cols(me)], recv_i.at[me], load_sem.at[8]),
    ]
    barrier = pltpu.get_barrier_semaphore()
    for k in range(1, n):
        pl.semaphore_signal(barrier, inc=1, device_id={"section": partner(me, k, n, 1)})
    for copy in loads:
        copy.start()

    def copies(kind, k, incoming=False):
        to = partner(me, k, n, 1)
        if kind == 0:
            src, dst = part, recv_p
        elif kind == 1:
            src, dst = hsend.at[to], recv_h
        elif kind == 2:
            src, dst = cs.at[:, cols(to)], recv_s
        else:
            src, dst = ci.at[:, cols(to)], recv_i
        slot = partner(me, k, n, -1) if incoming else me
        return pltpu.make_async_remote_copy(
            src_ref=src, dst_ref=dst.at[slot], send_sem=send_sem.at[kind, k],
            recv_sem=recv_sem.at[kind, slot], device_id={"section": to},
        )

    order = list(range(n // 2, n)) + list(range(n // 2 - 1, 0, -1))

    for copy in loads[:4]:
        copy.wait()
    start = start_ref[0]
    period = period_ref[0]

    row = lax.broadcasted_iota(jnp.int32, (n * SUB, 1), 0)
    late = row >= n * ITERS
    row = jnp.where(late, row - n * ITERS, row)
    block = row // ITERS - start
    block = jnp.where(block < 0, block + n, block)
    base = block * width
    item = row % ITERS
    ahead = base + jnp.minimum(period - base, width) + item
    ahead = jnp.where(ahead >= period, ahead - period, ahead)
    behind = base + item - ITERS
    behind = jnp.where(behind < 0, behind + period, behind)
    place = jnp.where(late, behind, ahead) + start * width
    place = jnp.where(place >= n * width, place - n * width, place)

    cpad[...] = jnp.zeros_like(cpad)

    def pick(j, total):
        at = pl.ds(pl.multiple_of(j * CHUNK, CHUNK), CHUNK)
        cpad[pl.ds(0, rs), :] = cs[:, at]
        cpad[pl.ds(rs, ri), :] = ci[:, at]
        column = lax.broadcasted_iota(jnp.int32, (n * SUB, CHUNK), 1) + j * CHUNK
        onehot = jnp.where(column == place, 1.0, 0.0).astype(jnp.bfloat16)
        rest = cpad[...]
        for _ in range(3):
            piece = rest.astype(jnp.bfloat16)
            rest = rest - piece.astype(jnp.float32)
            total = total + lax.dot_general(onehot, piece, NT, preferred_element_type=jnp.float32)
        return total

    picked = lax.fori_loop(
        0, cs.shape[1] // CHUNK, pick, jnp.zeros((n * SUB, LANES), jnp.float32)
    )
    packed = picked[:n * ITERS] + pltpu.roll(picked[n * ITERS:], half, 1)
    hsend[...] = packed.reshape(n, ITERS, LANES)
    recv_h[me] = hsend[me]

    pl.semaphore_wait(barrier, n - 1)
    for k in order:
        copies(1, k).start()
    for k in order:
        copies(2, k).start()
        copies(3, k).start()

    for copy in loads[4:7]:
        copy.wait()
    abt[...] = ab[...].T
    kt[...] = kkt[...].T
    link[pl.ds(0, SUB), :] = jnp.zeros((SUB, nx), jnp.float32)
    zn[pl.ds(rows, SUB), :] = jnp.zeros((SUB, nx), jnp.float32)

    mine = me - start
    mine = jnp.where(mine < 0, mine + n, mine)
    base = mine * width
    finish = jnp.minimum(period - base, width)

    for k in order:
        copies(1, k, True).wait_recv()

    lane = lax.broadcasted_iota(jnp.int32, (ITERS, LANES), 1)
    phase = (finish + 2 * width) % SUB
    for r, top in ((rs, 0), (ri, nx)):
        off = 0 if top == 0 else rs
        per = LANES // r
        for t in range(0, n * r, LANES):
            fore = jnp.zeros((ITERS, LANES), jnp.float32)
            aft = jnp.zeros((ITERS, LANES), jnp.float32)
            for q in range(min(per, n)):
                piece = recv_h[t // r + q]
                here = (lane >= q * r) & (lane < (q + 1) * r)
                fore = jnp.where(here, pltpu.roll(piece, (q * r - off) % LANES, 1), fore)
                aft = jnp.where(here, pltpu.roll(piece, (q * r - off - half) % LANES, 1), aft)
            at = pl.ds(top + t, LANES)
            hrow[pl.ds(0, ITERS), at] = -fore
            hrow[pl.ds(ITERS, ITERS), at] = -aft
    sub = lax.broadcasted_iota(jnp.int32, (SUB, 1), 0)
    negc[pl.ds(0, SUB), :] = jnp.where(sub >= ITERS, hrow[...], 0.0)
    for t in range(0, nw, LANES):
        at = pl.ds(t, LANES)
        ring = hrow[:, at]
        turned = ring
        for s in range(1, SUB):
            turned = jnp.where(phase == s, pltpu.roll(ring, s, 0), turned)
        hrow[:, at] = turned

    loads[7].wait()
    loads[8].wait()
    for k in order:
        copies(2, k, True).wait_recv()
        copies(3, k, True).wait_recv()

    def filled(r, value, at):
        ahead = sub + (r - SUB) - finish
        return jnp.where((ahead >= 0) & (ahead < ITERS), hrow[:, at], value)

    for r, top, src in ((rs, 0, recv_s), (ri, nx, recv_i)):
        per = LANES // r
        for t in range(0, n * r, LANES):
            at = pl.ds(top + t, LANES)
            for b in range(0, width, LANES):
                stack = [src[t // r + q, :, pl.ds(b, LANES)] for q in range(per)]
                turned = jnp.concatenate(stack, axis=0).T
                for i in range(0, LANES, SUB):
                    down = SUB + b + i
                    negc[pl.ds(down, SUB), at] = filled(down, -turned[i:i + SUB], at)
            negc[pl.ds(SUB + width, SUB), at] = filled(
                SUB + width, jnp.zeros((SUB, LANES), jnp.float32), at
            )

    for it in range(ITERS):
        last = it == ITERS - 1
        if it == 0:
            for r in range(0, rows, ROWS):
                at = pl.ds(r, ROWS)
                rhs[at, :] = negc[at, :].astype(jnp.bfloat16)
        else:
            for t in range(0, nw, TILE):
                to = pl.ds(t, TILE)
                w[:, to] = dot(g[...], ab[:, to])
                known = c if t < nx else negc
                for r in range(0, rows, ROWS):
                    at = pl.ds(r, ROWS)
                    rhs[at, to] = (known[at, to] + scaled(w[at, to])).astype(jnp.bfloat16)
        for t in range(0, nw, TILE):
            to = pl.ds(t, TILE)
            w[:, to] = dot(rhs[...], kt[:, to])
            for r in range(0, rows, ROWS):
                at = pl.ds(r, ROWS)
                wb[at, to] = w[at, to].astype(jnp.bfloat16)
        if last:
            primal = jnp.zeros((SUB, LANES), jnp.float32)
            dual = jnp.zeros((SUB, LANES), jnp.float32)
        for t in range(0, nx, TILE):
            to = pl.ds(t, TILE)
            pred[:, to] = dot(wb[...], abt[:, to])
            for r in range(0, rows, ROWS):
                at = pl.ds(r, ROWS)
                q = pred[at, to]
                link[pl.ds(SUB + r, ROWS), to] = q + v[at, to] if it else q
            for r in range(0, rows, ROWS):
                at = pl.ds(r, ROWS)
                x = w[at, to]
                own = x + y[at, to] if it else x
                znew = 0.5 * (own + link[pl.ds(SUB + r - 1, ROWS), to])
                zn[at, to] = znew
                if not last:
                    ynew = own - znew
                    y[at, to] = ynew
                    c[at, to] = negc[at, to] + scaled(znew - ynew)
                    if it == ITERS - 2:
                        z[at, to] = znew
            if not last:
                for r in range(0, rows, ROWS):
                    at = pl.ds(r, ROWS)
                    znext = zn[pl.ds(r + 1, ROWS), to]
                    vnew = link[pl.ds(SUB + r, ROWS), to] - znext
                    v[at, to] = vnew
                    g[at, to] = (znext - vnew).astype(jnp.bfloat16)
            else:
                for r in range(SUB, SUB + width, SUB):
                    at = pl.ds(r, SUB)
                    active = sub + (base + r - SUB) < period
                    znew = zn[at, to]
                    znext = zn[pl.ds(r + 1, SUB), to]
                    miss = (w[at, to] - znew) ** 2 + (pred[at, to] - znext) ** 2
                    change = znew - z[at, to]
                    miss = jnp.where(active, miss, 0.0)
                    change = jnp.where(active, change * change, 0.0)
                    for b in range(0, TILE, LANES):
                        primal = primal + miss[:, b:b + LANES]
                        dual = dual + change[:, b:b + LANES]

    part[pl.ds(0, 1), :] = jnp.sum(primal, axis=0, keepdims=True)
    part[pl.ds(1, 1), :] = RHO * RHO * jnp.sum(dual, axis=0, keepdims=True)
    recv_p[me] = part[...]
    for k in order:
        copies(0, k).start()

    for b in range(0, width, LANES):
        to = pl.ds(b, LANES)
        lane = lax.broadcasted_iota(jnp.int32, (1, LANES), 1)
        active = lane + (base + b) < period
        for t in range(0, nw, LANES):
            value = jnp.where(active, w[pl.ds(SUB + b, LANES), pl.ds(t, LANES)].T, 0.0)
            if t < nx:
                xo[pl.ds(t, LANES), to] = value
                zo[pl.ds(t, LANES), to] = jnp.where(
                    active, zn[pl.ds(SUB + b, LANES), pl.ds(t, LANES)].T, 0.0
                )
            else:
                uo[pl.ds(t - nx, LANES), to] = value
    outs = [
        pltpu.make_async_copy(xo, x_out, out_sem.at[0]),
        pltpu.make_async_copy(uo, u_out, out_sem.at[1]),
        pltpu.make_async_copy(zo, z_out, out_sem.at[2]),
    ]
    for copy in outs:
        copy.start()
    for k in order:
        copies(0, k, True).wait_recv()
    total = recv_p[0]
    for s in range(1, n):
        total = total + recv_p[s]
    top = jnp.sqrt(jnp.broadcast_to(jnp.sum(total[:1], keepdims=True), (SUB, LANES)))
    low = jnp.sqrt(jnp.broadcast_to(jnp.sum(total[1:], keepdims=True), (SUB, LANES)))
    norm_out[0] = jnp.max(top)
    norm_out[1] = jnp.max(low)
    for copy in outs:
        copy.wait()
    for kind in range(4):
        for k in order:
            copies(kind, k).wait_send()


def local(a, b, kkt, lin_state, lin_input, block_start, period):
    n = lax.axis_size("section")
    width = lin_state.shape[1] // n
    rows = width + 2 * SUB
    nx, nu = b.shape
    nw = nx + nu
    rs, ri = lin_state.shape[0], lin_input.shape[0]
    f32, bf16 = jnp.float32, jnp.bfloat16
    anyspec = pl.BlockSpec(memory_space=pl.ANY)
    smem = pl.BlockSpec(memory_space=pltpu.SMEM)
    vmem = pltpu.VMEM
    return pl.pallas_call(
        functools.partial(kernel, n, width),
        name="admm",
        out_shape=(
            jax.ShapeDtypeStruct((nx, width), f32),
            jax.ShapeDtypeStruct((nu, width), f32),
            jax.ShapeDtypeStruct((nx, width), f32),
            jax.ShapeDtypeStruct((2,), f32),
        ),
        in_specs=[anyspec] * 7,
        out_specs=(anyspec, anyspec, anyspec, smem),
        scratch_shapes=[
            vmem((nx, nw), bf16), vmem((nw, nx), bf16), vmem((nw, nw), bf16), vmem((nw, nw), bf16),
            vmem(lin_state.shape, f32), vmem(lin_input.shape, f32),
            vmem((n, rs, width), f32), vmem((n, ri, width), f32),
            vmem((LANES, CHUNK), f32),
            vmem((n, ITERS, LANES), f32), vmem((n, ITERS, LANES), f32), vmem((SUB, nw), f32),
            vmem((rows, nw), f32), vmem((rows, nw), bf16), vmem((rows, nw), f32),
            vmem((rows, nw), bf16), vmem((rows, nx), f32),
            vmem((rows + SUB, nx), f32), vmem((rows + SUB, nx), f32),
            vmem((rows, nx), f32), vmem((rows, nx), f32), vmem((rows, nx), f32), vmem((rows, nx), f32),
            vmem((rows, nx), bf16),
            vmem((nx, width), f32), vmem((nu, width), f32), vmem((nx, width), f32),
            vmem((2, LANES), f32), vmem((n, 2, LANES), f32),
            pltpu.SMEM((1,), jnp.int32), pltpu.SMEM((1,), jnp.int32),
            pltpu.SemaphoreType.DMA((9,)),
            pltpu.SemaphoreType.DMA((4, n)), pltpu.SemaphoreType.DMA((4, n)),
            pltpu.SemaphoreType.DMA((3,)),
        ],
        compiler_params=pltpu.CompilerParams(
            collective_id=0, has_side_effects=True, vmem_limit_bytes=62000000
        ),
    )(a, b, kkt, lin_state, lin_input, block_start, period)


def solution(mesh):
    return jax.shard_map(
        local,
        mesh=mesh,
        in_specs=(
            P("plant", None),
            P("plant", None),
            P("plant", None),
            P(("plant", "section"), None),
            P(("plant", "section"), None),
            P("plant"),
            P("plant"),
        ),
        out_specs=(P("plant", "section"), P("plant", "section"), P("plant", "section"), P("plant")),
        check_vma=False,
    )
```

time: 47.8 us -> 41.7 us (0.87)
  Pallas kernels: 41.7 us -> 35.6 us
    pallas_call x1, Pallas kernels: 41.7 us -> 35.6 us  [local(): pl.pallas_call(functools.partial(kernel, n, width), name='admm', out_shap...]
where the time goes in v1:
time: 41.7 us; the launch traced here: 41.5 us
  Pallas kernels  35.6 us (85%)
  local copies, waits for them, and re-layouts  3.96 us (9%)
  between operations  1.96 us (5%)
    pallas_call x1, Pallas kernels, local(): pl.pallas_call(functools.partial(kernel, n, width), name='admm', out_shap...  35.6 us
    unnamed x10, local copies, waits for them, and re-layouts  3.96 us

profile of v1, /device:TPU:0, one launch (start us, length us, event | category | flops | bytes accessed | tf_op | source)
XLA Modules:
  0.0 41.5 jit_solution(1918198117408030701)
XLA Ops:
  1.9 35.6 %admm.1 = (f32[512,256]{1,0:T(8,128)}, f32[256,256]{1,0:T(8,128)}, f32[512,256]{1,0:T(8,128)}, f32[2]{0:T(128)}) custom-call(bf16[512,512]{1,0:T(8,128)(2,1)} %a_hbm.1, bf16[512,256]{1,0:T(8,128)(2,1)} %b_hbm.1, bf16[768,768]{1,0:T(8,128)(2,1)} %k_hbm.1, f32[32,4096]{1,0:T(8,128)} %cs_hbm.1, f32[16,4096]{1,0:T(8,128)} %ci_hbm.1, s32[1]{0:T(128)S(6)} %copy.15.start_hbm, ...), custom_call_target="tpu_custom_call" | custom-call | tf_op jit(solution)/shard_map/admm/pallas_call | solution.py:322
  37.5 0.0 copy-start.1
  37.5 0.0 copy-start
  37.6 0.0 copy-start.2
  37.6 1.9 %copy.17 = f32[512,256]{1,0:T(8,128)} copy(f32[512,256]{1,0:T(8,128)} %get-tuple-element.8) | data formatting | bytes 1048576
  39.5 0.0 copy-done.1
  39.5 0.7 %copy.18 = f32[256,256]{1,0:T(8,128)} copy(f32[256,256]{1,0:T(8,128)S(1)} %copy-done.1) | data formatting | bytes 524288
  40.2 0.0 copy-done
  40.2 0.8 %copy.19 = f32[512,256]{1,0:T(8,128)} copy(f32[512,256]{1,0:T(8,128)S(1)} %copy-done) | data formatting | bytes 1048576
  41.0 0.0 copy-done.2
  41.0 0.5 %copy.20 = f32[2]{0:T(128)} copy(f32[2]{0:T(128)S(1)} %copy-done.2) | data formatting | bytes 16
Async XLA Ops:
  37.5 2.0 %copy-start.1 = (f32[256,256]{1,0:T(8,128)S(1)}, f32[256,256]{1,0:T(8,128)}, u32[]{:S(2)}) copy-start(f32[256,256]{1,0:T(8,128)} %get-tuple-element.9) | copy-start | bytes 786436
  37.5 2.7 %copy-start = (f32[512,256]{1,0:T(8,128)S(1)}, f32[512,256]{1,0:T(8,128)}, u32[]{:S(2)}) copy-start(f32[512,256]{1,0:T(8,128)} %get-tuple-element.10) | copy-start | bytes 1572868
  37.6 3.5 %copy-start.2 = (f32[2]{0:T(128)S(1)}, f32[2]{0:T(128)}, u32[]{:S(2)}) copy-start(f32[2]{0:T(128)} %get-tuple-element.11) | copy-start | bytes 28

commit v2 on v1

--- a/solution.py
+++ b/solution.py
@@ -37,12 +37,11 @@
 
 def kernel(
     n, width,
-    a_hbm, b_hbm, k_hbm, cs_hbm, ci_hbm, start_hbm, period_hbm,
-    x_out, u_out, z_out, norm_out,
+    a_hbm, b_hbm, k_hbm, cs_hbm, ci_hbm, start_ref, period_ref,
+    xo, uo, zo, norm_out,
     ab, abt, kkt, kt, cs, ci, recv_s, recv_i, cpad, hsend, recv_h, hrow,
-    negc, rhs, w, wb, pred, link, zn, y, v, c, z, g, xo, uo, zo, part, recv_p,
-    start_ref, period_ref,
-    load_sem, send_sem, recv_sem, out_sem,
+    negc, rhs, w, wb, pred, link, zn, y, v, c, z, g, part, recv_p,
+    load_sem, send_sem, recv_sem,
 ):
     me = lax.axis_index("section")
     nx = a_hbm.shape[0]
@@ -58,13 +57,11 @@
     loads = [
         pltpu.make_async_copy(cs_hbm, cs, load_sem.at[0]),
         pltpu.make_async_copy(ci_hbm, ci, load_sem.at[1]),
-        pltpu.make_async_copy(start_hbm, start_ref, load_sem.at[2]),
-        pltpu.make_async_copy(period_hbm, period_ref, load_sem.at[3]),
-        pltpu.make_async_copy(a_hbm, ab.at[:, pl.ds(0, nx)], load_sem.at[4]),
-        pltpu.make_async_copy(b_hbm, ab.at[:, pl.ds(nx, nu)], load_sem.at[5]),
-        pltpu.make_async_copy(k_hbm, kkt, load_sem.at[6]),
-        pltpu.make_async_copy(cs_hbm.at[:, cols(me)], recv_s.at[me], load_sem.at[7]),
-        pltpu.make_async_copy(ci_hbm.at[:, cols(me)], recv_i.at[me], load_sem.at[8]),
+        pltpu.make_async_copy(a_hbm, ab.at[:, pl.ds(0, nx)], load_sem.at[2]),
+        pltpu.make_async_copy(b_hbm, ab.at[:, pl.ds(nx, nu)], load_sem.at[3]),
+        pltpu.make_async_copy(k_hbm, kkt, load_sem.at[4]),
+        pltpu.make_async_copy(cs_hbm.at[:, cols(me)], recv_s.at[me], load_sem.at[5]),
+        pltpu.make_async_copy(ci_hbm.at[:, cols(me)], recv_i.at[me], load_sem.at[6]),
     ]
     barrier = pltpu.get_barrier_semaphore()
     for k in range(1, n):
@@ -90,7 +87,7 @@
 
     order = list(range(n // 2, n)) + list(range(n // 2 - 1, 0, -1))
 
-    for copy in loads[:4]:
+    for copy in loads[:2]:
         copy.wait()
     start = start_ref[0]
     period = period_ref[0]
@@ -138,7 +135,7 @@
         copies(2, k).start()
         copies(3, k).start()
 
-    for copy in loads[4:7]:
+    for copy in loads[2:5]:
         copy.wait()
     abt[...] = ab[...].T
     kt[...] = kkt[...].T
@@ -179,8 +176,8 @@
             turned = jnp.where(phase == s, pltpu.roll(ring, s, 0), turned)
         hrow[:, at] = turned
 
-    loads[7].wait()
-    loads[8].wait()
+    loads[5].wait()
+    loads[6].wait()
     for k in order:
         copies(2, k, True).wait_recv()
         copies(3, k, True).wait_recv()
@@ -285,13 +282,6 @@
                 )
             else:
                 uo[pl.ds(t - nx, LANES), to] = value
-    outs = [
-        pltpu.make_async_copy(xo, x_out, out_sem.at[0]),
-        pltpu.make_async_copy(uo, u_out, out_sem.at[1]),
-        pltpu.make_async_copy(zo, z_out, out_sem.at[2]),
-    ]
-    for copy in outs:
-        copy.start()
     for k in order:
         copies(0, k, True).wait_recv()
     total = recv_p[0]
@@ -301,11 +291,21 @@
     low = jnp.sqrt(jnp.broadcast_to(jnp.sum(total[1:], keepdims=True), (SUB, LANES)))
     norm_out[0] = jnp.max(top)
     norm_out[1] = jnp.max(low)
-    for copy in outs:
-        copy.wait()
     for kind in range(4):
         for k in order:
             copies(kind, k).wait_send()
+
+
+def store(*refs):
+    sem = refs[-1]
+    half = (len(refs) - 1) // 2
+    moves = [
+        pltpu.make_async_copy(refs[i], refs[half + i], sem.at[i]) for i in range(half)
+    ]
+    for move in moves:
+        move.start()
+    for move in moves:
+        move.wait()
 
 
 def local(a, b, kkt, lin_state, lin_input, block_start, period):
@@ -318,8 +318,14 @@
     f32, bf16 = jnp.float32, jnp.bfloat16
     anyspec = pl.BlockSpec(memory_space=pl.ANY)
     smem = pl.BlockSpec(memory_space=pltpu.SMEM)
+    vspec = pl.BlockSpec(memory_space=pltpu.VMEM)
+    hbm = pl.BlockSpec(memory_space=pltpu.HBM)
     vmem = pltpu.VMEM
-    return pl.pallas_call(
+    inputs = [
+        pltpu.with_memory_space_constraint(value, pltpu.HBM)
+        for value in (a, b, kkt, lin_state, lin_input)
+    ]
+    results = pl.pallas_call(
         functools.partial(kernel, n, width),
         name="admm",
         out_shape=(
@@ -328,8 +334,8 @@
             jax.ShapeDtypeStruct((nx, width), f32),
             jax.ShapeDtypeStruct((2,), f32),
         ),
-        in_specs=[anyspec] * 7,
-        out_specs=(anyspec, anyspec, anyspec, smem),
+        in_specs=[hbm] * 5 + [smem] * 2,
+        out_specs=(vspec, vspec, vspec, smem),
         scratch_shapes=[
             vmem((nx, nw), bf16), vmem((nw, nx), bf16), vmem((nw, nw), bf16), vmem((nw, nw), bf16),
             vmem(lin_state.shape, f32), vmem(lin_input.shape, f32),
@@ -341,17 +347,23 @@
             vmem((rows + SUB, nx), f32), vmem((rows + SUB, nx), f32),
             vmem((rows, nx), f32), vmem((rows, nx), f32), vmem((rows, nx), f32), vmem((rows, nx), f32),
             vmem((rows, nx), bf16),
-            vmem((nx, width), f32), vmem((nu, width), f32), vmem((nx, width), f32),
             vmem((2, LANES), f32), vmem((n, 2, LANES), f32),
-            pltpu.SMEM((1,), jnp.int32), pltpu.SMEM((1,), jnp.int32),
-            pltpu.SemaphoreType.DMA((9,)),
+            pltpu.SemaphoreType.DMA((7,)),
             pltpu.SemaphoreType.DMA((4, n)), pltpu.SemaphoreType.DMA((4, n)),
-            pltpu.SemaphoreType.DMA((3,)),
         ],
         compiler_params=pltpu.CompilerParams(
-            collective_id=0, has_side_effects=True, vmem_limit_bytes=62000000
+            collective_id=0, has_side_effects=True, vmem_limit_bytes=24000000
         ),
-    )(a, b, kkt, lin_state, lin_input, block_start, period)
+    )(*inputs, block_start, period)
+    return pl.pallas_call(
+        store,
+        name="store",
+        out_shape=tuple(jax.ShapeDtypeStruct(r.shape, r.dtype) for r in results),
+        in_specs=[anyspec] * 4,
+        out_specs=(anyspec,) * 4,
+        scratch_shapes=[pltpu.SemaphoreType.DMA((4,))],
+        compiler_params=pltpu.CompilerParams(vmem_limit_bytes=4000000),
+    )(*results)
 
 
 def solution(mesh):

time: 41.7 us -> 38.8 us (0.930)
  local copies, waits for them, and re-layouts: 3.96 us -> 0 us
  Pallas kernels: 35.6 us -> 36.7 us
    unnamed x10 -> x0, local copies, waits for them, and re-layouts: 3.96 us -> none
    pallas_call x0 -> x1, Pallas kernels: none -> 1.09 us  [local(): pl.pallas_call(store, name='store', out_shape=tuple((jax.ShapeDtypeStruct...]
where the time goes in v2:
time: 38.8 us; the launch traced here: 38.7 us
  Pallas kernels  36.7 us (95%)
  between operations  1.93 us (5%)
    pallas_call x1, Pallas kernels, local(): pl.pallas_call(functools.partial(kernel, n, width), name='admm', out_shap...  35.6 us
    pallas_call x1, Pallas kernels, local(): pl.pallas_call(store, name='store', out_shape=tuple((jax.ShapeDtypeStruct...  1.09 us

profile of v2, /device:TPU:0, one launch (start us, length us, event | category | flops | bytes accessed | tf_op | source)
XLA Modules:
  0.0 38.7 jit_solution(4030739168825362374)
XLA Ops:
  1.9 35.6 %admm.1 = (f32[512,256]{1,0:T(8,128)S(1)}, f32[256,256]{1,0:T(8,128)S(1)}, f32[512,256]{1,0:T(8,128)S(1)}, f32[2]{0:T(128)S(1)}) custom-call(bf16[512,512]{1,0:T(8,128)(2,1)} %a_hbm.1, bf16[512,256]{1,0:T(8,128)(2,1)} %b_hbm.1, bf16[768,768]{1,0:T(8,128)(2,1)} %k_hbm.1, f32[32,4096]{1,0:T(8,128)} %cs_hbm.1, f32[16,4096]{1,0:T(8,128)} %ci_hbm.1, ...), custom_call_target="tpu_custom_call" | custom-call | tf_op jit(solution)/shard_map/admm/pallas_call | solution.py:328
  37.6 1.1 %store.1 = (f32[512,256]{1,0:T(8,128)}, f32[256,256]{1,0:T(8,128)}, f32[512,256]{1,0:T(8,128)}, f32[2]{0:T(128)}) custom-call(f32[512,256]{1,0:T(8,128)S(1)} %get-tuple-element.8.refs_0_, f32[256,256]{1,0:T(8,128)S(1)} %get-tuple-element.9.refs_1_, f32[512,256]{1,0:T(8,128)S(1)} %get-tuple-element.10.refs_2_, f32[2]{0:T(128)S(1)} %get-tuple-element.11.refs_3_), custom_call_target="tpu_custom_call" | custom-call | tf_op jit(solution)/shard_map/store/pallas_call | solution.py:358

commit v3 on v2

--- a/solution.py
+++ b/solution.py
@@ -38,7 +38,7 @@
 def kernel(
     n, width,
     a_hbm, b_hbm, k_hbm, cs_hbm, ci_hbm, start_ref, period_ref,
-    xo, uo, zo, norm_out,
+    xo, uo, zo, total_out,
     ab, abt, kkt, kt, cs, ci, recv_s, recv_i, cpad, hsend, recv_h, hrow,
     negc, rhs, w, wb, pred, link, zn, y, v, c, z, g, part, recv_p,
     load_sem, send_sem, recv_sem,
@@ -287,25 +287,28 @@
     total = recv_p[0]
     for s in range(1, n):
         total = total + recv_p[s]
-    top = jnp.sqrt(jnp.broadcast_to(jnp.sum(total[:1], keepdims=True), (SUB, LANES)))
-    low = jnp.sqrt(jnp.broadcast_to(jnp.sum(total[1:], keepdims=True), (SUB, LANES)))
-    norm_out[0] = jnp.max(top)
-    norm_out[1] = jnp.max(low)
+    total_out[...] = total
     for kind in range(4):
         for k in order:
             copies(kind, k).wait_send()
 
 
-def store(*refs):
-    sem = refs[-1]
-    half = (len(refs) - 1) // 2
+def store(x, u, z, total, x_out, u_out, z_out, norm_out, norm, sem):
     moves = [
-        pltpu.make_async_copy(refs[i], refs[half + i], sem.at[i]) for i in range(half)
+        pltpu.make_async_copy(src, dst, sem.at[i])
+        for i, (src, dst) in enumerate(((x, x_out), (u, u_out), (z, z_out)))
     ]
     for move in moves:
         move.start()
+    both = jnp.sum(total[...], axis=1, keepdims=True)
+    both = jnp.sqrt(jnp.broadcast_to(both, (2, LANES)))
+    norm[0] = jnp.max(both[:1])
+    norm[1] = jnp.max(both[1:])
+    last = pltpu.make_async_copy(norm, norm_out, sem.at[3])
+    last.start()
     for move in moves:
         move.wait()
+    last.wait()
 
 
 def local(a, b, kkt, lin_state, lin_input, block_start, period):
@@ -332,10 +335,10 @@
             jax.ShapeDtypeStruct((nx, width), f32),
             jax.ShapeDtypeStruct((nu, width), f32),
             jax.ShapeDtypeStruct((nx, width), f32),
-            jax.ShapeDtypeStruct((2,), f32),
+            jax.ShapeDtypeStruct((2, LANES), f32),
         ),
         in_specs=[hbm] * 5 + [smem] * 2,
-        out_specs=(vspec, vspec, vspec, smem),
+        out_specs=(vspec,) * 4,
         scratch_shapes=[
             vmem((nx, nw), bf16), vmem((nw, nx), bf16), vmem((nw, nw), bf16), vmem((nw, nw), bf16),
             vmem(lin_state.shape, f32), vmem(lin_input.shape, f32),
@@ -358,10 +361,11 @@
     return pl.pallas_call(
         store,
         name="store",
-        out_shape=tuple(jax.ShapeDtypeStruct(r.shape, r.dtype) for r in results),
-        in_specs=[anyspec] * 4,
+        out_shape=tuple(jax.ShapeDtypeStruct(r.shape, f32) for r in results[:3])
+        + (jax.ShapeDtypeStruct((2,), f32),),
+        in_specs=[anyspec] * 3 + [vspec],
         out_specs=(anyspec,) * 4,
-        scratch_shapes=[pltpu.SemaphoreType.DMA((4,))],
+        scratch_shapes=[pltpu.SMEM((2,), f32), pltpu.SemaphoreType.DMA((4,))],
         compiler_params=pltpu.CompilerParams(vmem_limit_bytes=4000000),
     )(*results)
 

time: 38.8 us -> 38.1 us (0.982)
  Pallas kernels: 36.7 us -> 36 us
    pallas_call x1, Pallas kernels: 35.6 us -> 34.9 us  [local(): pl.pallas_call(functools.partial(kernel, n, width), name='admm', out_shap...]
where the time goes in v3:
time: 38.1 us; the launch traced here: 37.9 us
  Pallas kernels  36 us (94%)
  between operations  1.93 us (5%)
    pallas_call x1, Pallas kernels, local(): pl.pallas_call(functools.partial(kernel, n, width), name='admm', out_shap...  34.9 us
    pallas_call x1, Pallas kernels, local(): pl.pallas_call(store, name='store', out_shape=tuple((jax.ShapeDtypeStruct...  1.1 us

profile of v3, /device:TPU:0, one launch (start us, length us, event | category | flops | bytes accessed | tf_op | source)
XLA Modules:
  0.0 37.9 jit_solution(15134869147891185208)
XLA Ops:
  1.9 34.9 %admm.1 = (f32[512,256]{1,0:T(8,128)S(1)}, f32[256,256]{1,0:T(8,128)S(1)}, f32[512,256]{1,0:T(8,128)S(1)}, f32[2,128]{1,0:T(2,128)S(1)}) custom-call(bf16[512,512]{1,0:T(8,128)(2,1)} %a_hbm.1, bf16[512,256]{1,0:T(8,128)(2,1)} %b_hbm.1, bf16[768,768]{1,0:T(8,128)(2,1)} %k_hbm.1, f32[32,4096]{1,0:T(8,128)} %cs_hbm.1, f32[16,4096]{1,0:T(8,128)} %ci_hbm.1, ...), custom_call_target="tpu_custom_call" | custom-call | tf_op jit(solution)/shard_map/admm/pallas_call | solution.py:331
  36.8 1.1 %store.1 = (f32[512,256]{1,0:T(8,128)}, f32[256,256]{1,0:T(8,128)}, f32[512,256]{1,0:T(8,128)}, f32[2]{0:T(128)}) custom-call(f32[512,256]{1,0:T(8,128)S(1)} %get-tuple-element.8.x, f32[256,256]{1,0:T(8,128)S(1)} %get-tuple-element.9.u, f32[512,256]{1,0:T(8,128)S(1)} %get-tuple-element.10.z, f32[2,128]{1,0:T(2,128)S(1)} %get-tuple-element.11.total), custom_call_target="tpu_custom_call" | custom-call | tf_op jit(solution)/shard_map/store/pallas_call | solution.py:361

commit v4 on v3

--- a/solution.py
+++ b/solution.py
@@ -178,17 +178,26 @@
 
     loads[5].wait()
     loads[6].wait()
-    for k in order:
-        copies(2, k, True).wait_recv()
-        copies(3, k, True).wait_recv()
+    def arrived(kind, slot):
+        src, dst = ((cs, recv_s), (ci, recv_i))[kind - 2]
+
+        @pl.when(slot != me)
+        def _():
+            pltpu.make_async_remote_copy(
+                src_ref=src.at[:, cols(slot)], dst_ref=dst.at[slot],
+                send_sem=send_sem.at[kind, 0], recv_sem=recv_sem.at[kind, slot],
+                device_id={"section": slot},
+            ).wait_recv()
 
     def filled(r, value, at):
         ahead = sub + (r - SUB) - finish
         return jnp.where((ahead >= 0) & (ahead < ITERS), hrow[:, at], value)
 
-    for r, top, src in ((rs, 0, recv_s), (ri, nx, recv_i)):
+    for kind, r, top, src in ((2, rs, 0, recv_s), (3, ri, nx, recv_i)):
         per = LANES // r
         for t in range(0, n * r, LANES):
+            for q in range(per):
+                arrived(kind, t // r + q)
             at = pl.ds(top + t, LANES)
             for b in range(0, width, LANES):
                 stack = [src[t // r + q, :, pl.ds(b, LANES)] for q in range(per)]

time: 38.1 us -> 38.1 us (level)
  no operation moved by 1% of the time
where the time goes in v4:
time: 38.1 us; the launch traced here: 38 us
  Pallas kernels  36 us (94%)
  between operations  1.93 us (5%)
    pallas_call x1, Pallas kernels, local(): pl.pallas_call(functools.partial(kernel, n, width), name='admm', out_shap...  34.9 us
    pallas_call x1, Pallas kernels, local(): pl.pallas_call(store, name='store', out_shape=tuple((jax.ShapeDtypeStruct...  1.1 us

profile of v4, /device:TPU:0, one launch (start us, length us, event | category | flops | bytes accessed | tf_op | source)
XLA Modules:
  0.0 38.0 jit_solution(5495928836038572231)
XLA Ops:
  1.9 34.9 %admm.1 = (f32[512,256]{1,0:T(8,128)S(1)}, f32[256,256]{1,0:T(8,128)S(1)}, f32[512,256]{1,0:T(8,128)S(1)}, f32[2,128]{1,0:T(2,128)S(1)}) custom-call(bf16[512,512]{1,0:T(8,128)(2,1)} %a_hbm.1, bf16[512,256]{1,0:T(8,128)(2,1)} %b_hbm.1, bf16[768,768]{1,0:T(8,128)(2,1)} %k_hbm.1, f32[32,4096]{1,0:T(8,128)} %cs_hbm.1, f32[16,4096]{1,0:T(8,128)} %ci_hbm.1, ...), custom_call_target="tpu_custom_call" | custom-call | tf_op jit(solution)/shard_map/admm/pallas_call | solution.py:340
  36.9 1.1 %store.1 = (f32[512,256]{1,0:T(8,128)}, f32[256,256]{1,0:T(8,128)}, f32[512,256]{1,0:T(8,128)}, f32[2]{0:T(128)}) custom-call(f32[512,256]{1,0:T(8,128)S(1)} %get-tuple-element.8.x, f32[256,256]{1,0:T(8,128)S(1)} %get-tuple-element.9.u, f32[512,256]{1,0:T(8,128)S(1)} %get-tuple-element.10.z, f32[2,128]{1,0:T(2,128)S(1)} %get-tuple-element.11.total), custom_call_target="tpu_custom_call" | custom-call | tf_op jit(solution)/shard_map/store/pallas_call | solution.py:370
